TPU v7x, 32 devices: a whole 2x2x4 slice. The times are simulated.
32 devices in a mesh: groups: 2 (over y), tx: 4 (over z), ty: 2 (over x), ka: 2 (over core).
Axes of the slice: x: 2, y: 2, z: 4, core: 2. Of those that a mesh axis runs over, the one named last changes fastest.
Arguments:
- mask_raster: float32 [2048, 512], P(('groups', 'tx'), 'ty'), parts along dimension 0, may hold values from 0 to 1
- frag_rows: int32 [8, 2, 512], P(('groups', 'tx'), 'ty'), parts along dimension 0, may hold values from 8 to 215
- frag_cols: int32 [8, 2, 512], P(('groups', 'tx'), 'ty'), parts along dimension 0, may hold values from 8 to 215
- frag_length: int32 [8, 2, 512], P(('groups', 'tx'), 'ty'), parts along dimension 0, may hold values from 4 to 32
- frag_orient: int32 [8, 2, 512], P(('groups', 'tx'), 'ty'), parts along dimension 0, may hold values from 0 to 1
- frag_moves: int32 [8, 2, 2, 512], P(('groups', 'tx'), 'ty'), parts along dimension 0, may hold values from -4 to 4
- site_rows: int32 [8, 2, 2048], P(('groups', 'tx'), 'ty'), parts along dimension 0, may hold values from 1 to 254
- site_cols: int32 [8, 2, 2048], P(('groups', 'tx'), 'ty'), parts along dimension 0, may hold values from 1 to 254
- spectra: float32 [16, 2, 128, 128], P('ka'), may hold values from -24 to 24
- weights: float32 [16], P('ka'), may hold values from 0.05 to 1
- tolerance: int32 [2], replicated, may hold values from 1 to 16
Outputs:
- intensity: float32 [2048, 512], P(('groups', 'tx'), 'ty'), parts along dimension 0
- corrected_mask: float32 [2048, 512], P(('groups', 'tx'), 'ty'), parts along dimension 0
- edge_errors: float32 [8, 2, 2, 2048], P(('groups', 'tx'), 'ty'), parts along dimension 0
- peak_error: float32 [4], P('groups'), parts along dimension 0
- converged_share: float32 [4], P('groups'), parts along dimension 0
There are 2 independent parts, one for each index of `groups`. A program takes and returns all parts, laid end to end along the dimension named above; an argument that names none is the same for every part. Nothing has to cross between parts.
All inputs are finite; a program needn't handle non-finite values.
Results may differ from a plain program's by a relative error of at most 0.0003.
Values sent between devices are 32-bit elements; how exact they have to be, the bound alone decides.
No kernel may reach another device: no remote copies, remote signals or barrier semaphores. Data moves between devices by JAX's collectives and lax.ppermute only.
A program may use at most 64 MiB of HBM per device.

v0:
```python
import functools
import math

import jax
import jax.numpy as jnp
import numpy as np
from jax import lax
from jax.experimental import pallas as pl
from jax.experimental.pallas import tpu as pltpu
from jax.sharding import PartitionSpec as P

HALO = 128
BAND = 128
ITERS = 2

LEVEL = 0.4
SLOPE_FLOOR = 0.05
SHARPNESS = 8.0

F32 = jnp.float32
BF16 = jnp.bfloat16
VMEM = pltpu.MemorySpace.VMEM
SMEM = pltpu.MemorySpace.SMEM
PAD_ROWS = 16
LIMIT = pltpu.CompilerParams(vmem_limit_bytes=24 * 1024 * 1024)


def terms(x):
    high = x.astype(BF16)
    rest = x - high.astype(F32)
    mid = rest.astype(BF16)
    return high, mid, (rest - mid.astype(F32)).astype(BF16)


def table_terms(table):
    out = []
    for _ in range(3):
        part = table.astype(np.float32).astype(BF16)
        out.append(part)
        table = table - part.astype(np.float64)
    return out


@functools.lru_cache(maxsize=None)
def tables(tile):
    ext = tile + 2 * HALO
    half = BAND // 2
    rows = (BAND + 1 + PAD_ROWS - 1) // PAD_ROWS * PAD_ROWS
    step = 2.0 * math.pi / ext
    place = np.arange(ext) - (ext - 1) / 2
    freq = np.arange(BAND) - half

    def angle(freqs, places):
        return freqs[:, None] * places[None, :] * step

    forward_rows = np.zeros((rows, ext))
    forward_rows[: half + 1] = np.cos(angle(np.arange(half + 1), place))
    forward_rows[half + 1 : BAND + 1] = -np.sin(angle(np.arange(1, half + 1), place))
    turn = angle(place, freq)
    forward_cols = np.concatenate([np.cos(turn), np.sin(turn)], axis=1)
    expand = np.zeros((2 * BAND, rows))
    for index, f in enumerate(freq):
        expand[index, abs(f)] = 1.0
        if f != 0:
            expand[BAND + index, half + abs(f)] = np.sign(f)
    inner = angle(np.arange(tile // 2) + 0.5, freq)
    high, mid, low = table_terms(np.concatenate([np.cos(inner), np.sin(inner)]) / ext)
    inverse_rows = [np.concatenate(p, axis=1) for p in ((high, high), (mid, mid), (low, high))]
    inverse_cols = [np.ascontiguousarray(part.T) for part in inverse_rows]
    unfold = np.zeros((tile, tile))
    for j in range(tile // 2):
        unfold[tile // 2 + j, j] = 1.0
        unfold[tile // 2 - 1 - j, tile // 2 + j] = 1.0
    unfold = unfold.astype(np.float32).astype(BF16)
    return (
        table_terms(forward_rows),
        table_terms(forward_cols),
        expand.astype(np.float32).astype(BF16),
        inverse_rows,
        inverse_cols,
        [unfold, np.ascontiguousarray(unfold.T)],
    )


def mm(a, b):
    return jnp.dot(a, b, preferred_element_type=F32)


def mm6(a, b):
    small = mm(a[2], b[0]) + mm(a[0], b[2]) + mm(a[1], b[1])
    return small + mm(a[1], b[0]) + mm(a[0], b[1]) + mm(a[0], b[0])


def strips_body(mask, rows, cols, length, orient, moves, corrected, current, send_a, send_b):
    tile = mask.shape[0]
    frags = rows.shape[2]
    first = lax.axis_index("ka") == 0
    even = lax.axis_index("tx") % 2 == 0
    place = lax.broadcasted_iota(jnp.int32, (tile, frags), 0)
    row_start = rows[0]
    col_start = cols[0]
    size = length[0]
    along_rows = orient[0] == 0
    state = mask[...]
    states = []
    for iteration in range(ITERS):
        shift = moves[0, 0, iteration : iteration + 1, :]
        lower = jnp.minimum(shift, 0)
        upper = jnp.maximum(shift, 0)
        row_low = jnp.where(along_rows, row_start, row_start + lower)
        row_high = jnp.where(along_rows, row_start + size, row_start + upper)
        col_low = jnp.where(along_rows, col_start + lower, col_start)
        col_high = jnp.where(along_rows, col_start + upper, col_start + size)
        sign = jnp.where(shift > 0, 1.0, jnp.where(shift < 0, -1.0, 0.0))
        in_rows = jnp.where((place >= row_low) & (place < row_high), sign, 0.0)
        in_cols = jnp.where((place >= col_low) & (place < col_high), 1.0, 0.0)
        strips = lax.dot_general(
            in_rows.astype(BF16),
            in_cols.astype(BF16),
            (((1,), (1,)), ((), ())),
            preferred_element_type=F32,
        )
        state = jnp.clip(state + strips, 0.0, 1.0)
        states.append(state)
    corrected[...] = states[1]
    mine = jnp.where(first, states[0], states[1])
    current[...] = mine
    top = mine[:HALO]
    bottom = mine[tile - HALO :]
    send_a[...] = jnp.where(even, bottom, top)
    send_b[...] = jnp.where(even, top, bottom)


def prepare_body(*refs, count):
    anchor, weights, weights_other, tolerance, site_rows, site_cols = refs[:6]
    tables_in = refs[6 : 6 + count]
    chosen, rows_out, scales, limits = refs[6 + count : 10 + count]
    tables_out = refs[10 + count : 10 + 2 * count]
    sems = refs[-1]
    copies = [
        pltpu.make_async_copy(source, target, sems.at[i])
        for i, (source, target) in enumerate(zip(tables_in, tables_out))
    ]
    for copy in copies:
        copy.start()
    which = lax.axis_index("ka")
    kernels = weights.shape[0]
    lanes = scales.shape[1]
    for k in range(kernels):
        scales[k : k + 1, :] = jnp.full((1, lanes), weights[k])
        scales[kernels + k : kernels + k + 1, :] = jnp.full((1, lanes), weights_other[k])
    limits[...] = jnp.full(limits.shape, tolerance[which].astype(F32) / 8.0)
    rows_out[...] = site_rows[...]
    place = lax.broadcasted_iota(jnp.int32, chosen.shape, 0)
    chosen[...] = jnp.where(place == site_cols[0], 1.0, 0.0).astype(BF16)
    for copy in copies:
        copy.wait()


def rows_body(current, got_a, got_b, high, mid, low, out, send_a, send_b):
    tile = current.shape[1]
    even = lax.axis_index("tx") % 2 == 0
    even_col = lax.axis_index("ty") % 2 == 0
    above = jnp.where(even, got_b[...], got_a[...])
    below = jnp.where(even, got_a[...], got_b[...])
    extended = jnp.concatenate([above, current[...], below], axis=0)
    result = mm6((high[...], mid[...], low[...]), terms(extended))
    out[...] = result
    left = result[:, :HALO]
    right = result[:, tile - HALO :]
    send_a[...] = jnp.where(even_col, right, left)
    send_b[...] = jnp.where(even_col, left, right)


def image_body(
    mine,
    got_a,
    got_b,
    spec_own,
    spec_other,
    scales,
    site_rows,
    chosen,
    limits,
    cols_high,
    cols_mid,
    cols_low,
    expand,
    inv_rows_a,
    inv_rows_b,
    inv_rows_c,
    inv_cols_a,
    inv_cols_b,
    inv_cols_c,
    unfold_rows,
    unfold_cols,
    pack,
    stats,
    image,
):
    tile = mine.shape[1]
    half = tile // 2
    even_col = lax.axis_index("ty") % 2 == 0
    left = jnp.where(even_col, got_b[...], got_a[...])
    right = jnp.where(even_col, got_a[...], got_b[...])
    window = jnp.concatenate([left, mine[...], right], axis=1)
    half_spec = terms(mm6(terms(window), (cols_high[...], cols_mid[...], cols_low[...])))
    quads = sum(mm(expand[...], part) for part in reversed(half_spec))
    spec_re = quads[:BAND, :BAND] + quads[BAND:, BAND:]
    spec_im = quads[BAND:, :BAND] - quads[:BAND, BAND:]
    count = spec_own.shape[0]
    sources = [(spec_own, k) for k in range(count)] + [(spec_other, k) for k in range(count)]
    for number, (spec, k) in enumerate(sources):
        kr = spec[k, 0]
        ki = spec[k, 1]
        product = jnp.concatenate(
            [kr * spec_re - ki * spec_im, kr * spec_im + ki * spec_re], axis=1
        )
        high, mid, low = terms(product)
        first = jnp.concatenate([high, mid], axis=0)
        second = jnp.concatenate([high, low], axis=0)
        inner = mm(inv_rows_c[...], second) + mm(inv_rows_b[...], first) + mm(inv_rows_a[...], first)
        even_re = inner[:half, :BAND]
        even_im = inner[:half, BAND:]
        odd_re = inner[half:, :BAND]
        odd_im = inner[half:, BAND:]
        folded = jnp.concatenate(
            [even_re - odd_im, even_re + odd_im, even_im + odd_re, even_im - odd_re], axis=0
        )
        high, mid, low = terms(folded)
        first = jnp.concatenate([high, mid], axis=1)
        second = jnp.concatenate([high, low], axis=1)
        field = mm(second, inv_cols_c[...]) + mm(first, inv_cols_b[...]) + mm(first, inv_cols_a[...])
        even_re = field[:tile, :half]
        odd_re = field[:tile, half:]
        even_im = field[tile:, :half]
        odd_im = field[tile:, half:]
        forth_re = even_re - odd_im
        forth_im = even_im + odd_re
        back_re = even_re + odd_im
        back_im = even_im - odd_re
        weight = scales[number : number + 1, :]
        forth = weight * (forth_re * forth_re + forth_im * forth_im)
        back = weight * (back_re * back_re + back_im * back_im)
        if number == 0:
            image[:, :half] = forth
            image[:, half:] = back
        else:
            image[:, :half] += forth
            image[:, half:] += back
    picture = sum(mm(unfold_rows[...], part) for part in reversed(terms(image[...])))
    picture = sum(mm(part, unfold_cols[...]) for part in reversed(terms(picture)))
    pack[:tile, :] = picture
    grad_rows = (pltpu.roll(picture, tile - 1, 0) - pltpu.roll(picture, 1, 0)) * 0.5
    grad_cols = (pltpu.roll(picture, tile - 1, 1) - pltpu.roll(picture, 1, 1)) * 0.5
    slope = jnp.sqrt(grad_rows * grad_rows + grad_cols * grad_cols)
    errors = terms((picture - LEVEL) / jnp.maximum(slope, SLOPE_FLOOR))
    sites = site_rows.shape[2]
    place = lax.broadcasted_iota(jnp.int32, (tile, tile), 0)
    limit = limits[...][0:1, 0:1]
    peak = None
    for j in range(sites // tile):
        lanes = slice(j * tile, (j + 1) * tile)
        sampled = mm(errors[0], chosen[:, lanes]) + mm(errors[1], chosen[:, lanes])
        found = jnp.sum(
            jnp.where(place == site_rows[0, :, lanes], sampled, 0.0), axis=0, keepdims=True
        )
        pack[tile + j : tile + j + 1, :] = found
        size = jnp.abs(found)
        share = 1.0 / (1.0 + jnp.exp(SHARPNESS * (size - limit)))
        if peak is None:
            peak, shares = size, share
        else:
            peak, shares = jnp.maximum(peak, size), shares + share
    lane = lax.broadcasted_iota(jnp.int32, stats.shape, 1)
    stats[...] = jnp.where(lane == 0, jnp.max(peak), jnp.sum(shares))


def final_body(pack, other, stats, intensity, errors, peaks, shares, *, total):
    tile = pack.shape[1]
    first = lax.axis_index("ka") == 0
    intensity[...] = jnp.where(first, other[:tile, :], pack[:tile, :])
    mine = pack[tile:, :]
    theirs = other[tile:, :]
    zero = jnp.where(first, mine, theirs)
    one = jnp.where(first, theirs, mine)
    for j in range(errors.shape[3] // tile):
        lanes = slice(j * tile, (j + 1) * tile)
        errors[0, 0, 0:1, lanes] = zero[j : j + 1]
        errors[0, 0, 1:2, lanes] = one[j : j + 1]
    got = stats[...]
    iteration = lax.broadcasted_iota(jnp.int32, got.shape, 0) % ITERS
    lane = lax.broadcasted_iota(jnp.int32, got.shape, 1)
    for t in range(ITERS):
        peaks[t] = jnp.max(jnp.where((iteration == t) & (lane == 0), got, 0.0))
        shares[t] = jnp.sum(jnp.where((iteration == t) & (lane == 1), got, 0.0)) / total


def spec(count, space=VMEM):
    return [pl.BlockSpec(memory_space=space)] * count


def in_hbm(x):
    return pltpu.with_memory_space_constraint(x, pltpu.MemorySpace.HBM)


def shape(*dims):
    return jax.ShapeDtypeStruct(dims, F32)


def neighbours(axis, send_a, send_b):
    count = lax.axis_size(axis)
    got = []
    for start, sent in ((0, send_a), (1, send_b)):
        pairs = [(i, i + 1) for i in range(start, count - 1, 2)]
        if pairs:
            got.append(lax.ppermute(sent, axis, pairs + [(b, a) for a, b in pairs]))
        else:
            got.append(jnp.zeros_like(sent))
    return got


def shards(
    mask_raster,
    frag_rows,
    frag_cols,
    frag_length,
    frag_orient,
    frag_moves,
    site_rows,
    site_cols,
    spectra,
    weights,
    tolerance,
):
    tile = mask_raster.shape[0]
    sites = site_rows.shape[2]
    fwd_rows, fwd_cols, expand, inv_rows, inv_cols, unfold = tables(tile)
    half_rows = fwd_rows[0].shape[0]
    swap = [(0, 1), (1, 0)]
    spectra_other = lax.ppermute(spectra, "ka", swap)
    weights_other = lax.ppermute(weights, "ka", swap)
    corrected, current, send_a, send_b = pl.pallas_call(
        strips_body,
        out_shape=[shape(tile, tile), shape(tile, tile), shape(HALO, tile), shape(HALO, tile)],
        in_specs=spec(6),
        out_specs=spec(4),
        compiler_params=LIMIT,
        name="strips",
    )(*map(in_hbm, (mask_raster, frag_rows, frag_cols, frag_length, frag_orient, frag_moves)))
    got_a, got_b = neighbours("tx", send_a, send_b)
    constants = [*fwd_rows, *fwd_cols, expand, *inv_rows, *inv_cols, *unfold]
    members = lax.axis_size("tx") * lax.axis_size("ty") * lax.axis_size("ka")
    kernels = spectra.shape[0] * lax.axis_size("ka")
    chosen, rows_at, scales, limits, *constants = pl.pallas_call(
        functools.partial(prepare_body, count=len(constants)),
        out_shape=[
            jax.ShapeDtypeStruct((tile, sites), BF16),
            jax.ShapeDtypeStruct(site_rows.shape, jnp.int32),
            shape(kernels, 128),
            shape(8, 128),
        ]
        + [jax.ShapeDtypeStruct(c.shape, BF16) for c in constants],
        in_specs=spec(1, pl.ANY) + spec(3, SMEM) + spec(2) + spec(len(constants), pl.ANY),
        out_specs=spec(4 + len(constants)),
        scratch_shapes=[pltpu.SemaphoreType.DMA((len(constants),))],
        compiler_params=LIMIT,
        name="prepare",
    )(
        send_a,
        weights,
        weights_other,
        tolerance,
        in_hbm(site_rows),
        in_hbm(site_cols),
        *[in_hbm(jnp.asarray(c)) for c in constants],
    )
    mine, send_a, send_b = pl.pallas_call(
        rows_body,
        out_shape=[shape(half_rows, tile), shape(half_rows, HALO), shape(half_rows, HALO)],
        in_specs=spec(6),
        out_specs=spec(3),
        compiler_params=LIMIT,
        name="rows",
    )(current, got_a, got_b, *constants[:3])
    got_a, got_b = neighbours("ty", send_a, send_b)
    pack_rows = tile + sites // tile
    pack, stats = pl.pallas_call(
        image_body,
        out_shape=[shape(pack_rows, tile), shape(members, 128)],
        in_specs=spec(9 + len(constants) - 3),
        out_specs=spec(2),
        scratch_shapes=[pltpu.VMEM((tile, tile), F32)],
        compiler_params=LIMIT,
        name="image",
    )(
        mine,
        got_a,
        got_b,
        spectra,
        spectra_other,
        scales,
        rows_at,
        chosen,
        limits,
        *constants[3:],
    )
    other = lax.ppermute(pack, "ka", swap)
    merged = lax.all_to_all(stats, ("tx", "ty", "ka"), 0, 0, tiled=True)
    total = float(sites * lax.axis_size("tx") * lax.axis_size("ty"))
    intensity, errors, peaks, shares = pl.pallas_call(
        functools.partial(final_body, total=total),
        out_shape=[shape(tile, tile), shape(1, 1, ITERS, sites), shape(ITERS), shape(ITERS)],
        in_specs=spec(3),
        out_specs=spec(2) + spec(2, SMEM),
        compiler_params=LIMIT,
        name="final",
    )(pack, other, merged)
    return (intensity, corrected, errors, peaks, shares)


def solution(mesh):
    assert mesh.shape["ka"] == ITERS
    placed = (
        P(("groups", "tx"), "ty"),
        P(("groups", "tx"), "ty", None),
        P(("groups", "tx"), "ty", None),
        P(("groups", "tx"), "ty", None),
        P(("groups", "tx"), "ty", None),
        P(("groups", "tx"), "ty", None, None),
        P(("groups", "tx"), "ty", None),
        P(("groups", "tx"), "ty", None),
        P("ka", None, None, None),
        P("ka"),
        P(),
    )
    return jax.shard_map(
        shards,
        mesh=mesh,
        in_specs=placed,
        out_specs=(
            P(("groups", "tx"), "ty"),
            P(("groups", "tx"), "ty"),
            P(("groups", "tx"), "ty", None, None),
            P("groups"),
            P("groups"),
        ),
        check_vma=False,
    )
```

profile of v0, /device:TPU:0, one launch (start us, length us, event | category | flops | bytes accessed | tf_op | source)
XLA Modules:
  0.0 40.2 jit_solution(2532388436428346196)
XLA Ops:
  0.6 0.6 %collective-permute-start.4 = (f32[8,2,128,128]{3,2,1,0:T(8,128)}, f32[8,2,128,128]{3,2,1,0:T(8,128)S(1)}, u32[]{:S(2)}, u32[]{:S(2)}) collective-permute-start(f32[8,2,128,128]{3,2,1,0:T(8,128)} %spec_own.1), channel_id=1, source_target_pairs={{0,1},{1,0},{2,3},{3,2},{4,5},{5,4},{6,7},{7,6},{8,9},{9,8},{10,11... | collective-permute-start | bytes 3145736 | tf_op jit(solution)/shard_map/ppermute | solution.py:341
  1.2 2.1 %strips.1 = (f32[256,256]{1,0:T(8,128)}, f32[256,256]{1,0:T(8,128)S(1)}, f32[128,256]{1,0:T(8,128)S(1)}, f32[128,256]{1,0:T(8,128)S(1)}) custom-call(f32[256,256]{1,0:T(8,128)} %mask.1, s32[1,1,512]{2,1,0:T(1,128)} %rows.2, s32[1,1,512]{2,1,0:T(1,128)} %cols.1, s32[1,1,512]{2,1,0:T(1,128)} %length.1, s32[1,1,512]{2,1,0:T(1,128)} %orient.1, ...), custom_call_target="tpu_custom_call" | custom-call | tf_op jit(solution)/shard_map/strips/pallas_call | solution.py:343
  3.3 0.0 copy-start.1
  3.3 0.0 copy-start.2
  3.3 2.6 %collective-permute-start = (f32[128,256]{1,0:T(8,128)S(1)}, f32[128,256]{1,0:T(8,128)S(1)}, u32[]{:S(2)}, u32[]{:S(2)}) collective-permute-start(f32[128,256]{1,0:T(8,128)S(1)} %get-tuple-element.37.refs_0_), channel_id=1, source_target_pairs={{0,4},{8,12},{4,0},{12,8},{1,5},{9,13},{5,1},{13,9},{2,6},{10,14},... | collective-permute-start | bytes 393224 | tf_op jit(solution)/shard_map/ppermute | solution.py:317
  5.9 0.7 %collective-permute-start.1 = (f32[128,256]{1,0:T(8,128)S(1)}, f32[128,256]{1,0:T(8,128)S(1)}, u32[]{:S(2)}, u32[]{:S(2)}) collective-permute-start(f32[128,256]{1,0:T(8,128)S(1)} %get-tuple-element.38), channel_id=1, source_target_pairs={{4,8},{8,4},{5,9},{9,5},{6,10},{10,6},{7,11},{11,7},{20,24},{24,20... | collective-permute-start | bytes 393224 | tf_op jit(solution)/shard_map/ppermute | solution.py:317
  6.6 0.0 copy-done.1
  6.6 0.3 collective-permute-start.2
  6.9 0.9 %collective-permute-done.2.refs_2_ = f32[8]{0:T(128)S(1)} collective-permute-done((f32[8]{0:T(128)S(1)}, f32[8]{0:T(128)S(1)}, u32[]{:S(2)}, u32[]{:S(2)}) %collective-permute-start.2) | collective-permute-done | bytes 64 | tf_op jit(solution)/shard_map/ppermute | solution.py:342
  7.8 0.0 copy-done.2
  7.8 2.5 %prepare.1 = (bf16[256,2048]{1,0:T(8,128)(2,1)S(1)}, s32[1,1,2048]{2,1,0:T(1,128)S(1)}, f32[16,128]{1,0:T(8,128)S(1)}, f32[8,128]{1,0:T(8,128)S(1)}, bf16[144,51...) custom-call(f32[128,256]{1,0:T(8,128)S(1)} %get-tuple-element.37.ref, ...), custom_call_target="tpu_custom_call" | custom-call | tf_op jit(solution)/shard_map/prepare/pallas_call | solution.py:355
  10.4 0.0 copy-start
  10.4 0.0 collective-permute-done.got_a
  10.4 0.0 collective-permute-done.1.got_b
  10.4 1.1 %rows.3 = (f32[144,256]{1,0:T(8,128)S(1)}, f32[144,128]{1,0:T(8,128)S(1)}, f32[144,128]{1,0:T(8,128)}) custom-call(f32[256,256]{1,0:T(8,128)S(1)} %get-tuple-element.36.current, f32[128,256]{1,0:T(8,128)S(1)} %collective-permute-done.got_a, f32[128,256]{1,0:T(8,128)S(1)} %collective-permute-done.1.got_b, bf16[144,512]{1,0:T(8,128)(2,1)S(1)} %get-tuple-element.39.high, ...), custom_call_target="tpu_custom_call" | custom-call | tf_op jit(solution)/shard_map/rows/pallas_call | solution.py:378
  11.5 1.5 %collective-permute-start.3 = (f32[144,128]{1,0:T(8,128)S(1)}, f32[144,128]{1,0:T(8,128)S(1)}, u32[]{:S(2)}, u32[]{:S(2)}) collective-permute-start(f32[144,128]{1,0:T(8,128)S(1)} %get-tuple-element.43), channel_id=1, source_target_pairs={{0,2},{2,0},{1,3},{3,1},{4,6},{6,4},{5,7},{7,5},{8,10},{10,8},{9,1... | collective-permute-start | bytes 221192 | tf_op jit(solution)/shard_map/ppermute | solution.py:317
  13.0 2.9 %collective-permute-done.3.got_a = f32[144,128]{1,0:T(8,128)S(1)} collective-permute-done((f32[144,128]{1,0:T(8,128)S(1)}, f32[144,128]{1,0:T(8,128)S(1)}, u32[]{:S(2)}, u32[]{:S(2)}) %collective-permute-start.3) | collective-permute-done | bytes 73760 | tf_op jit(solution)/shard_map/ppermute | solution.py:317
  15.9 0.0 collective-permute-done.4.spec_other
  15.9 0.0 copy-done
  15.9 9.3 %image.1 = (f32[264,256]{1,0:T(8,128)S(1)}, f32[16,128]{1,0:T(8,128)S(1)}) custom-call(f32[144,256]{1,0:T(8,128)S(1)} %get-tuple-element.42.mine, f32[144,128]{1,0:T(8,128)S(1)} %collective-permute-done.3.got_a, f32[144,128]{1,0:T(8,128)S(1)} %broadcast_in_dim.3.got_b, f32[8,2,128,128]{3,2,1,0:T(8,128)S(1)} %copy-done, ...), custom_call_target="tpu_custom_call" | custom-call | tf_op jit(solution)/shard_map/image/pallas_call | solution.py:388
  25.2 0.1 collective-permute-start.5
  25.2 14.2 %all_to_all.11 = f32[16,1,128]{2,1,0:T(1,128)S(1)} all-to-all(f32[16,1,128]{2,1,0:T(1,128)S(1)} %bitcast.5), channel_id=1, replica_groups=mesh['groups'=2,'tx'=4,'ty'=2,'ka'=2] {'tx','ty','ka'}, dimensions={0} | all-to-all | bytes 16384 | tf_op jit(solution)/shard_map/all_to_all | solution.py:409
  39.4 0.0 collective-permute-done.5.other
  39.4 0.8 %final.1 = (f32[256,256]{1,0:T(8,128)}, f32[1,1,2,2048]{3,2,1,0:T(2,128)}, f32[2]{0:T(128)}, f32[2]{0:T(128)}) custom-call(f32[264,256]{1,0:T(8,128)S(1)} %get-tuple-element.60.pack, f32[264,256]{1,0:T(8,128)S(1)} %collective-permute-done.5.other, f32[16,128]{1,0:T(8,128)S(1)} %bitcast.4), custom_call_target="tpu_custom_call" | custom-call | tf_op jit(solution)/shard_map/final/pallas_call | solution.py:411
  (1 shorter events, 0.0 us)
Async XLA Ops:
  0.6 15.2 %collective-permute-start.4 = (f32[8,2,128,128]{3,2,1,0:T(8,128)}, f32[8,2,128,128]{3,2,1,0:T(8,128)S(1)}, u32[]{:S(2)}, u32[]{:S(2)}) collective-permute-start(f32[8,2,128,128]{3,2,1,0:T(8,128)} %spec_own.1), channel_id=1, source_target_pairs={{0,1},{1,0},{2,3},{3,2},{4,5},{5,4},{6,7},{7,6},{8,9},{9,8},{10,11... | collective-permute-start | bytes 3145736 | tf_op jit(solution)/shard_map/ppermute | solution.py:341
  3.3 3.2 %copy-start.1 = (f32[8]{0:T(128)S(1)}, f32[8]{0:T(128)}, u32[]{:S(2)}) copy-start(f32[8]{0:T(128)} %refs_1_.1) | copy-start | bytes 100
  3.3 4.5 %copy-start.2 = (s32[2]{0:T(128)S(1)}, s32[2]{0:T(128)}, u32[]{:S(2)}) copy-start(s32[2]{0:T(128)} %refs_3_.1) | copy-start | bytes 28
  3.3 7.0 %collective-permute-start = (f32[128,256]{1,0:T(8,128)S(1)}, f32[128,256]{1,0:T(8,128)S(1)}, u32[]{:S(2)}, u32[]{:S(2)}) collective-permute-start(f32[128,256]{1,0:T(8,128)S(1)} %get-tuple-element.37.refs_0_), channel_id=1, source_target_pairs={{0,4},{8,12},{4,0},{12,8},{1,5},{9,13},{5,1},{13,9},{2,6},{10,14},... | collective-permute-start | bytes 393224 | tf_op jit(solution)/shard_map/ppermute | solution.py:317
  5.9 4.5 %collective-permute-start.1 = (f32[128,256]{1,0:T(8,128)S(1)}, f32[128,256]{1,0:T(8,128)S(1)}, u32[]{:S(2)}, u32[]{:S(2)}) collective-permute-start(f32[128,256]{1,0:T(8,128)S(1)} %get-tuple-element.38), channel_id=1, source_target_pairs={{4,8},{8,4},{5,9},{9,5},{6,10},{10,6},{7,11},{11,7},{20,24},{24,20... | collective-permute-start | bytes 393224 | tf_op jit(solution)/shard_map/ppermute | solution.py:317
  6.6 1.2 %collective-permute-start.2 = (f32[8]{0:T(128)S(1)}, f32[8]{0:T(128)S(1)}, u32[]{:S(2)}, u32[]{:S(2)}) collective-permute-start(f32[8]{0:T(128)S(1)} %copy-done.1), channel_id=1, source_target_pairs={{0,1},{1,0},{2,3},{3,2},{4,5},{5,4},{6,7},{7,6},{8,9},{9,8},{10,11... | collective-permute-start | bytes 104 | tf_op jit(solution)/shard_map/ppermute | solution.py:342
  10.4 5.5 %copy-start = (f32[8,2,128,128]{3,2,1,0:T(8,128)S(1)}, f32[8,2,128,128]{3,2,1,0:T(8,128)}, u32[]{:S(2)}) copy-start(f32[8,2,128,128]{3,2,1,0:T(8,128)} %spec_own.1) | copy-start | bytes 3145732
  11.5 4.4 %collective-permute-start.3 = (f32[144,128]{1,0:T(8,128)S(1)}, f32[144,128]{1,0:T(8,128)S(1)}, u32[]{:S(2)}, u32[]{:S(2)}) collective-permute-start(f32[144,128]{1,0:T(8,128)S(1)} %get-tuple-element.43), channel_id=1, source_target_pairs={{0,2},{2,0},{1,3},{3,1},{4,6},{6,4},{5,7},{7,5},{8,10},{10,8},{9,1... | collective-permute-start | bytes 221192 | tf_op jit(solution)/shard_map/ppermute | solution.py:317
  25.2 14.3 %collective-permute-start.5 = (f32[264,256]{1,0:T(8,128)S(1)}, f32[264,256]{1,0:T(8,128)S(1)}, u32[]{:S(2)}, u32[]{:S(2)}) collective-permute-start(f32[264,256]{1,0:T(8,128)S(1)} %get-tuple-element.60.pack), channel_id=1, source_target_pairs={{0,1},{1,0},{2,3},{3,2},{4,5},{5,4},{6,7},{7,6},{8,9},{9,8},{10,11... | collective-permute-start | bytes 811016 | tf_op jit(solution)/shard_map/ppermute | solution.py:408
where the time goes:
time: 40.5 us; the launch traced here: 40.2 us
  Pallas kernels  15.8 us (39%)
  blocking collectives  14.2 us (35%)
  starting transfers between devices  5.63 us (14%)
  waiting for transfers between devices  3.85 us (10%)
  between operations  0.71 us (2%)
    all_to_all x1, blocking collectives, shards(): merged = lax.all_to_all(stats, ('tx', 'ty', 'ka'), 0, 0, tiled=True)  14.2 us
    pallas_call x1, Pallas kernels, shards(): pl.pallas_call(image_body, out_shape=[shape(pack_rows, tile), shape(membe...  9.27 us
    ppermute x3, starting transfers between devices, neighbours(): got.append(lax.ppermute(sent, axis, pairs + [(b, a) for a, b in pairs]))  4.73 us
    ppermute x3, waiting for transfers between devices, neighbours(): got.append(lax.ppermute(sent, axis, pairs + [(b, a) for a, b in pairs]))  2.9 us
    pallas_call x1, Pallas kernels, shards(): pl.pallas_call(functools.partial(prepare_body, count=len(constants)), out...  2.53 us
    pallas_call x1, Pallas kernels, shards(): pl.pallas_call(strips_body, out_shape=[shape(tile, tile), shape(tile, til...  2.14 us
    pallas_call x1, Pallas kernels, shards(): pl.pallas_call(rows_body, out_shape=[shape(half_rows, tile), shape(half_r...  1.09 us
    ppermute x1, waiting for transfers between devices, shards(): weights_other = lax.ppermute(weights, 'ka', swap)  0.95 us
  transfers between devices with their start and end apart: 6, of which 2 were waited for; matrix products, arithmetic and copies ran while one was open for 0% of the time, Pallas kernels for 14%

commit v1 on v0

--- a/solution.py
+++ b/solution.py
@@ -8,6 +8,7 @@
 from jax.experimental import pallas as pl
 from jax.experimental.pallas import tpu as pltpu
 from jax.sharding import PartitionSpec as P
+
 
 HALO = 128
 BAND = 128
@@ -131,11 +132,31 @@
     send_b[...] = jnp.where(even, top, bottom)
 
 
-def prepare_body(*refs, count):
-    anchor, weights, weights_other, tolerance, site_rows, site_cols = refs[:6]
-    tables_in = refs[6 : 6 + count]
-    chosen, rows_out, scales, limits = refs[6 + count : 10 + count]
-    tables_out = refs[10 + count : 10 + 2 * count]
+def prepare_rows_body(anchor, weights, spectra, *refs, count):
+    tables_in = refs[:count]
+    scaled = refs[count]
+    tables_out = refs[count + 1 : 2 * count + 1]
+    sems = refs[-1]
+    copies = [
+        pltpu.make_async_copy(source, target, sems.at[i])
+        for i, (source, target) in enumerate(zip([spectra, *tables_in], [scaled, *tables_out]))
+    ]
+    for copy in copies:
+        copy.start()
+    copies[0].wait()
+    lanes = scaled.shape[3]
+    for k in range(scaled.shape[0]):
+        factor = jnp.sqrt(jnp.full((1, 1, lanes), weights[k]))
+        scaled[k] = scaled[k] * factor
+    for copy in copies[1:]:
+        copy.wait()
+
+
+def prepare_image_body(*refs, count):
+    _, tolerance, site_rows, site_cols = refs[:4]
+    tables_in = refs[4 : 4 + count]
+    chosen, rows_out, limits = refs[4 + count : 7 + count]
+    tables_out = refs[7 + count : 7 + 2 * count]
     sems = refs[-1]
     copies = [
         pltpu.make_async_copy(source, target, sems.at[i])
@@ -144,11 +165,6 @@
     for copy in copies:
         copy.start()
     which = lax.axis_index("ka")
-    kernels = weights.shape[0]
-    lanes = scales.shape[1]
-    for k in range(kernels):
-        scales[k : k + 1, :] = jnp.full((1, lanes), weights[k])
-        scales[kernels + k : kernels + k + 1, :] = jnp.full((1, lanes), weights_other[k])
     limits[...] = jnp.full(limits.shape, tolerance[which].astype(F32) / 8.0)
     rows_out[...] = site_rows[...]
     place = lax.broadcasted_iota(jnp.int32, chosen.shape, 0)
@@ -178,7 +194,6 @@
     got_b,
     spec_own,
     spec_other,
-    scales,
     site_rows,
     chosen,
     limits,
@@ -239,9 +254,8 @@
         forth_im = even_im + odd_re
         back_re = even_re + odd_im
         back_im = even_im - odd_re
-        weight = scales[number : number + 1, :]
-        forth = weight * (forth_re * forth_re + forth_im * forth_im)
-        back = weight * (back_re * back_re + back_im * back_im)
+        forth = forth_re * forth_re + forth_im * forth_im
+        back = back_re * back_re + back_im * back_im
         if number == 0:
             image[:, :half] = forth
             image[:, half:] = back
@@ -338,8 +352,6 @@
     fwd_rows, fwd_cols, expand, inv_rows, inv_cols, unfold = tables(tile)
     half_rows = fwd_rows[0].shape[0]
     swap = [(0, 1), (1, 0)]
-    spectra_other = lax.ppermute(spectra, "ka", swap)
-    weights_other = lax.ppermute(weights, "ka", swap)
     corrected, current, send_a, send_b = pl.pallas_call(
         strips_body,
         out_shape=[shape(tile, tile), shape(tile, tile), shape(HALO, tile), shape(HALO, tile)],
@@ -349,46 +361,53 @@
         name="strips",
     )(*map(in_hbm, (mask_raster, frag_rows, frag_cols, frag_length, frag_orient, frag_moves)))
     got_a, got_b = neighbours("tx", send_a, send_b)
-    constants = [*fwd_rows, *fwd_cols, expand, *inv_rows, *inv_cols, *unfold]
-    members = lax.axis_size("tx") * lax.axis_size("ty") * lax.axis_size("ka")
-    kernels = spectra.shape[0] * lax.axis_size("ka")
-    chosen, rows_at, scales, limits, *constants = pl.pallas_call(
-        functools.partial(prepare_body, count=len(constants)),
+    scaled, *row_tables = pl.pallas_call(
+        functools.partial(prepare_rows_body, count=len(fwd_rows)),
+        out_shape=[shape(*spectra.shape)]
+        + [jax.ShapeDtypeStruct(c.shape, BF16) for c in fwd_rows],
+        in_specs=spec(1, pl.ANY) + spec(1, SMEM) + spec(1 + len(fwd_rows), pl.ANY),
+        out_specs=spec(1 + len(fwd_rows)),
+        scratch_shapes=[pltpu.SemaphoreType.DMA((1 + len(fwd_rows),))],
+        compiler_params=LIMIT,
+        name="prepare_rows",
+    )(send_a, weights, in_hbm(spectra), *[in_hbm(jnp.asarray(c)) for c in fwd_rows])
+    scaled_other = lax.ppermute(scaled, "ka", swap)
+    mine, send_a, send_b = pl.pallas_call(
+        rows_body,
+        out_shape=[shape(half_rows, tile), shape(half_rows, HALO), shape(half_rows, HALO)],
+        in_specs=spec(6),
+        out_specs=spec(3),
+        compiler_params=LIMIT,
+        name="rows",
+    )(current, got_a, got_b, *row_tables)
+    got_a, got_b = neighbours("ty", send_a, send_b)
+    constants = [*fwd_cols, expand, *inv_rows, *inv_cols, *unfold]
+    chosen, rows_at, limits, *constants = pl.pallas_call(
+        functools.partial(prepare_image_body, count=len(constants)),
         out_shape=[
             jax.ShapeDtypeStruct((tile, sites), BF16),
             jax.ShapeDtypeStruct(site_rows.shape, jnp.int32),
-            shape(kernels, 128),
             shape(8, 128),
         ]
         + [jax.ShapeDtypeStruct(c.shape, BF16) for c in constants],
-        in_specs=spec(1, pl.ANY) + spec(3, SMEM) + spec(2) + spec(len(constants), pl.ANY),
-        out_specs=spec(4 + len(constants)),
+        in_specs=spec(1, pl.ANY) + spec(1, SMEM) + spec(2) + spec(len(constants), pl.ANY),
+        out_specs=spec(3 + len(constants)),
         scratch_shapes=[pltpu.SemaphoreType.DMA((len(constants),))],
         compiler_params=LIMIT,
-        name="prepare",
+        name="prepare_image",
     )(
         send_a,
-        weights,
-        weights_other,
         tolerance,
         in_hbm(site_rows),
         in_hbm(site_cols),
         *[in_hbm(jnp.asarray(c)) for c in constants],
     )
-    mine, send_a, send_b = pl.pallas_call(
-        rows_body,
-        out_shape=[shape(half_rows, tile), shape(half_rows, HALO), shape(half_rows, HALO)],
-        in_specs=spec(6),
-        out_specs=spec(3),
-        compiler_params=LIMIT,
-        name="rows",
-    )(current, got_a, got_b, *constants[:3])
-    got_a, got_b = neighbours("ty", send_a, send_b)
+    members = lax.axis_size("tx") * lax.axis_size("ty") * lax.axis_size("ka")
     pack_rows = tile + sites // tile
     pack, stats = pl.pallas_call(
         image_body,
         out_shape=[shape(pack_rows, tile), shape(members, 128)],
-        in_specs=spec(9 + len(constants) - 3),
+        in_specs=spec(8 + len(constants)),
         out_specs=spec(2),
         scratch_shapes=[pltpu.VMEM((tile, tile), F32)],
         compiler_params=LIMIT,
@@ -397,13 +416,12 @@
         mine,
         got_a,
         got_b,
-        spectra,
-        spectra_other,
-        scales,
+        scaled,
+        scaled_other,
         rows_at,
         chosen,
         limits,
-        *constants[3:],
+        *constants,
     )
     other = lax.ppermute(pack, "ka", swap)
     merged = lax.all_to_all(stats, ("tx", "ty", "ka"), 0, 0, tiled=True)

time: 40.5 us -> 42.2 us (1.042)
  blocking collectives: 14.2 us -> 10.4 us
  starting transfers between devices: 5.63 us -> 8.24 us
  Pallas kernels: 15.8 us -> 17.5 us
  local copies, waits for them, and re-layouts: 0.02 us -> 0.66 us
  waiting for transfers between devices: 3.85 us -> 4.44 us
    all_to_all x1, blocking collectives: 14.2 us -> 10.4 us  [shards(): merged = lax.all_to_all(stats, ('tx', 'ty', 'ka'), 0, 0, tiled=True)]
    ppermute x3, starting transfers between devices: 4.73 us -> 7.61 us  [neighbours(): got.append(lax.ppermute(sent, axis, pairs + [(b, a) for a, b in pairs]))]
    pallas_call x1 -> x2, Pallas kernels: 2.53 us -> 4.17 us  [the longest x1 2.28 us: shards(): pl.pallas_call(functools.partial(prepare_image_body, count=len(constants)...]
    ppermute x3, waiting for transfers between devices: 2.9 us -> 4.44 us  [neighbours(): got.append(lax.ppermute(sent, axis, pairs + [(b, a) for a, b in pairs]))]
    ppermute x2 -> x1, waiting for transfers between devices: 0.95 us -> 0.01 us  [shards(): scaled_other = lax.ppermute(scaled, 'ka', swap)]
    unnamed x6 -> x4, local copies, waits for them, and re-layouts: 0.01 us -> 0.66 us
  transfers between devices with their start and end apart: 6 -> 5, of which waited for: 2 -> 2; matrix products, arithmetic and copies ran while one was open for 0% -> 0% of each run, Pallas kernels for 14% -> 8%
where the time goes in v1:
time: 42.2 us; the launch traced here: 41.9 us
  Pallas kernels  17.5 us (41%)
  blocking collectives  10.4 us (25%)
  starting transfers between devices  8.24 us (20%)
  waiting for transfers between devices  4.44 us (11%)
  between operations  0.68 us (2%)
  local copies, waits for them, and re-layouts  0.66 us (2%)
    all_to_all x1, blocking collectives, shards(): merged = lax.all_to_all(stats, ('tx', 'ty', 'ka'), 0, 0, tiled=True)  10.4 us
    pallas_call x1, Pallas kernels, shards(): pl.pallas_call(image_body, out_shape=[shape(pack_rows, tile), shape(membe...  9.35 us
    ppermute x3, starting transfers between devices, neighbours(): got.append(lax.ppermute(sent, axis, pairs + [(b, a) for a, b in pairs]))  7.61 us
    ppermute x3, waiting for transfers between devices, neighbours(): got.append(lax.ppermute(sent, axis, pairs + [(b, a) for a, b in pairs]))  4.44 us
    pallas_call x1, Pallas kernels, shards(): pl.pallas_call(functools.partial(prepare_image_body, count=len(constants)...  2.28 us
    pallas_call x1, Pallas kernels, shards(): pl.pallas_call(strips_body, out_shape=[shape(tile, tile), shape(tile, til...  2.14 us
    pallas_call x1, Pallas kernels, shards(): pl.pallas_call(functools.partial(prepare_rows_body, count=len(fwd_rows)),...  1.89 us
    pallas_call x1, Pallas kernels, shards(): pl.pallas_call(rows_body, out_shape=[shape(half_rows, tile), shape(half_r...  1.08 us
  transfers between devices with their start and end apart: 5, of which 2 were waited for; matrix products, arithmetic and copies ran while one was open for 0% of the time, Pallas kernels for 8%

profile of v1, /device:TPU:0, one launch (start us, length us, event | category | flops | bytes accessed | tf_op | source)
XLA Modules:
  0.0 41.9 jit_solution(3230289732478205421)
XLA Ops:
  0.6 2.1 %strips.1 = (f32[256,256]{1,0:T(8,128)}, f32[256,256]{1,0:T(8,128)S(1)}, f32[128,256]{1,0:T(8,128)S(1)}, f32[128,256]{1,0:T(8,128)S(1)}) custom-call(f32[256,256]{1,0:T(8,128)} %mask.1, s32[1,1,512]{2,1,0:T(1,128)} %rows.2, s32[1,1,512]{2,1,0:T(1,128)} %cols.1, s32[1,1,512]{2,1,0:T(1,128)} %length.1, s32[1,1,512]{2,1,0:T(1,128)} %orient.1, ...), custom_call_target="tpu_custom_call" | custom-call | tf_op jit(solution)/shard_map/strips/pallas_call | solution.py:355
  2.8 0.0 copy-start
  2.8 0.7 %copy-done = f32[8]{0:T(128)S(1)} copy-done((f32[8]{0:T(128)S(1)}, f32[8]{0:T(128)}, u32[]{:S(2)}) %copy-start) | copy-done | bytes 56
  3.4 1.9 %prepare_rows.1 = (f32[8,2,128,128]{3,2,1,0:T(8,128)S(1)}, bf16[144,512]{1,0:T(8,128)(2,1)S(1)}, bf16[144,512]{1,0:T(8,128)(2,1)S(1)}, bf16[144,512]{1,0:T(8,128)(2,1)S(1)}) custom-call(f32[128,256]{1,0:T(8,128)S(1)} %get-tuple-element.37.anchor, f32[8]{0:T(128)S(1)} %copy-done, f32[8,2,128,128]{3,2,1,0:T(8,128)} %spectra.1, ...), custom_call_target="tpu_custom_call" | custom-call | tf_op jit(solution)/shard_map/prepare_rows/pallas_call | solution.py:364
  5.3 0.6 %collective-permute-start.3 = (f32[8,2,128,128]{3,2,1,0:T(8,128)S(1)}, f32[8,2,128,128]{3,2,1,0:T(8,128)S(1)}, u32[]{:S(2)}, u32[]{:S(2)}) collective-permute-start(f32[8,2,128,128]{3,2,1,0:T(8,128)S(1)} %get-tuple-element.44.spec_own), channel_id=1, source_target_pairs={{0,1},{1,0},{2,3},{3,2},{4,5},{5,4},{6,7},{7,6},{8,9},{9,8},{10,11... | collective-permute-start | bytes 3145736 | tf_op jit(solution)/shard_map/ppermute | solution.py:374
  5.9 0.7 %collective-permute-start.1 = (f32[128,256]{1,0:T(8,128)S(1)}, f32[128,256]{1,0:T(8,128)S(1)}, u32[]{:S(2)}, u32[]{:S(2)}) collective-permute-start(f32[128,256]{1,0:T(8,128)S(1)} %get-tuple-element.38), channel_id=1, source_target_pairs={{4,8},{8,4},{5,9},{9,5},{6,10},{10,6},{7,11},{11,7},{20,24},{24,20... | collective-permute-start | bytes 393224 | tf_op jit(solution)/shard_map/ppermute | solution.py:331
  6.5 5.5 %collective-permute-start = (f32[128,256]{1,0:T(8,128)S(1)}, f32[128,256]{1,0:T(8,128)S(1)}, u32[]{:S(2)}, u32[]{:S(2)}) collective-permute-start(f32[128,256]{1,0:T(8,128)S(1)} %get-tuple-element.37.anchor), channel_id=1, source_target_pairs={{0,4},{8,12},{4,0},{12,8},{1,5},{9,13},{5,1},{13,9},{2,6},{10,14},... | collective-permute-start | bytes 393224 | tf_op jit(solution)/shard_map/ppermute | solution.py:331
  12.0 0.0 collective-permute-done.1.got_b
  12.0 3.9 %collective-permute-done.got_a = f32[128,256]{1,0:T(8,128)S(1)} collective-permute-done((f32[128,256]{1,0:T(8,128)S(1)}, f32[128,256]{1,0:T(8,128)S(1)}, u32[]{:S(2)}, u32[]{:S(2)}) %collective-permute-start) | collective-permute-done | bytes 131104 | tf_op jit(solution)/shard_map/ppermute | solution.py:331
  15.9 1.1 %rows.3 = (f32[144,256]{1,0:T(8,128)S(1)}, f32[144,128]{1,0:T(8,128)S(1)}, f32[144,128]{1,0:T(8,128)}) custom-call(f32[256,256]{1,0:T(8,128)S(1)} %get-tuple-element.36.current, f32[128,256]{1,0:T(8,128)S(1)} %collective-permute-done.got_a, f32[128,256]{1,0:T(8,128)S(1)} %collective-permute-done.1.got_b, bf16[144,512]{1,0:T(8,128)(2,1)S(1)} %get-tuple-element.39.high, ...), custom_call_target="tpu_custom_call" | custom-call | tf_op jit(solution)/shard_map/rows/pallas_call | solution.py:375
  17.0 0.0 copy-start.1
  17.0 1.5 %collective-permute-start.2 = (f32[144,128]{1,0:T(8,128)S(1)}, f32[144,128]{1,0:T(8,128)S(1)}, u32[]{:S(2)}, u32[]{:S(2)}) collective-permute-start(f32[144,128]{1,0:T(8,128)S(1)} %get-tuple-element.43.refs_0_), channel_id=1, source_target_pairs={{0,2},{2,0},{1,3},{3,1},{4,6},{6,4},{5,7},{7,5},{8,10},{10,8},{9,1... | collective-permute-start | bytes 221192 | tf_op jit(solution)/shard_map/ppermute | solution.py:331
  18.4 0.0 copy-done.1
  18.5 2.3 %prepare_image.1 = (bf16[256,2048]{1,0:T(8,128)(2,1)S(1)}, s32[1,1,2048]{2,1,0:T(1,128)S(1)}, f32[8,128]{1,0:T(8,128)S(1)}, bf16[512,256]{1,0:T(8,128)(2,1)S(1)}...) custom-call(f32[144,128]{1,0:T(8,128)S(1)} %get-tuple-element.43.ref, ...), custom_call_target="tpu_custom_call" | custom-call | tf_op jit(solution)/shard_map/prepare_image/pallas_call | solution.py:385
  20.7 0.6 %collective-permute-done.2.got_a = f32[144,128]{1,0:T(8,128)S(1)} collective-permute-done((f32[144,128]{1,0:T(8,128)S(1)}, f32[144,128]{1,0:T(8,128)S(1)}, u32[]{:S(2)}, u32[]{:S(2)}) %collective-permute-start.2) | collective-permute-done | bytes 73760 | tf_op jit(solution)/shard_map/ppermute | solution.py:331
  21.3 0.0 collective-permute-done.3.spec_other
  21.3 9.3 %image.1 = (f32[264,256]{1,0:T(8,128)S(1)}, f32[16,128]{1,0:T(8,128)S(1)}) custom-call(f32[144,256]{1,0:T(8,128)S(1)} %get-tuple-element.42.mine, f32[144,128]{1,0:T(8,128)S(1)} %collective-permute-done.2.got_a, f32[144,128]{1,0:T(8,128)S(1)} %broadcast_in_dim.3.got_b, f32[8,2,128,128]{3,2,1,0:T(8,128)S(1)} %get-tuple-element.44.spec_own, ...), custom_call_target="tpu_custom_call" | custom-call | tf_op jit(solution)/shard_map/image/pallas_call | solution.py:407
  30.7 0.1 collective-permute-start.4
  30.8 10.4 %all_to_all.11 = f32[16,1,128]{2,1,0:T(1,128)S(1)} all-to-all(f32[16,1,128]{2,1,0:T(1,128)S(1)} %bitcast.5), channel_id=1, replica_groups=mesh['groups'=2,'tx'=4,'ty'=2,'ka'=2] {'tx','ty','ka'}, dimensions={0} | all-to-all | bytes 16384 | tf_op jit(solution)/shard_map/all_to_all | solution.py:427
  41.1 0.0 collective-permute-done.4.other
  41.1 0.8 %final.1 = (f32[256,256]{1,0:T(8,128)}, f32[1,1,2,2048]{3,2,1,0:T(2,128)}, f32[2]{0:T(128)}, f32[2]{0:T(128)}) custom-call(f32[264,256]{1,0:T(8,128)S(1)} %get-tuple-element.60.pack, f32[264,256]{1,0:T(8,128)S(1)} %collective-permute-done.4.other, f32[16,128]{1,0:T(8,128)S(1)} %bitcast.4), custom_call_target="tpu_custom_call" | custom-call | tf_op jit(solution)/shard_map/final/pallas_call | solution.py:429
  (1 shorter events, 0.0 us)
Async XLA Ops:
  2.8 0.7 %copy-start = (f32[8]{0:T(128)S(1)}, f32[8]{0:T(128)}, u32[]{:S(2)}) copy-start(f32[8]{0:T(128)} %weights.1) | copy-start | bytes 100
  5.3 16.0 %collective-permute-start.3 = (f32[8,2,128,128]{3,2,1,0:T(8,128)S(1)}, f32[8,2,128,128]{3,2,1,0:T(8,128)S(1)}, u32[]{:S(2)}, u32[]{:S(2)}) collective-permute-start(f32[8,2,128,128]{3,2,1,0:T(8,128)S(1)} %get-tuple-element.44.spec_own), channel_id=1, source_target_pairs={{0,1},{1,0},{2,3},{3,2},{4,5},{5,4},{6,7},{7,6},{8,9},{9,8},{10,11... | collective-permute-start | bytes 3145736 | tf_op jit(solution)/shard_map/ppermute | solution.py:374
  5.9 6.1 %collective-permute-start.1 = (f32[128,256]{1,0:T(8,128)S(1)}, f32[128,256]{1,0:T(8,128)S(1)}, u32[]{:S(2)}, u32[]{:S(2)}) collective-permute-start(f32[128,256]{1,0:T(8,128)S(1)} %get-tuple-element.38), channel_id=1, source_target_pairs={{4,8},{8,4},{5,9},{9,5},{6,10},{10,6},{7,11},{11,7},{20,24},{24,20... | collective-permute-start | bytes 393224 | tf_op jit(solution)/shard_map/ppermute | solution.py:331
  6.5 9.3 %collective-permute-start = (f32[128,256]{1,0:T(8,128)S(1)}, f32[128,256]{1,0:T(8,128)S(1)}, u32[]{:S(2)}, u32[]{:S(2)}) collective-permute-start(f32[128,256]{1,0:T(8,128)S(1)} %get-tuple-element.37.anchor), channel_id=1, source_target_pairs={{0,4},{8,12},{4,0},{12,8},{1,5},{9,13},{5,1},{13,9},{2,6},{10,14},... | collective-permute-start | bytes 393224 | tf_op jit(solution)/shard_map/ppermute | solution.py:331
  17.0 1.5 %copy-start.1 = (s32[2]{0:T(128)S(1)}, s32[2]{0:T(128)}, u32[]{:S(2)}) copy-start(s32[2]{0:T(128)} %refs_1_.2) | copy-start | bytes 28
  17.0 4.4 %collective-permute-start.2 = (f32[144,128]{1,0:T(8,128)S(1)}, f32[144,128]{1,0:T(8,128)S(1)}, u32[]{:S(2)}, u32[]{:S(2)}) collective-permute-start(f32[144,128]{1,0:T(8,128)S(1)} %get-tuple-element.43.refs_0_), channel_id=1, source_target_pairs={{0,2},{2,0},{1,3},{3,1},{4,6},{6,4},{5,7},{7,5},{8,10},{10,8},{9,1... | collective-permute-start | bytes 221192 | tf_op jit(solution)/shard_map/ppermute | solution.py:331
  30.7 10.5 %collective-permute-start.4 = (f32[264,256]{1,0:T(8,128)S(1)}, f32[264,256]{1,0:T(8,128)S(1)}, u32[]{:S(2)}, u32[]{:S(2)}) collective-permute-start(f32[264,256]{1,0:T(8,128)S(1)} %get-tuple-element.60.pack), channel_id=1, source_target_pairs={{0,1},{1,0},{2,3},{3,2},{4,5},{5,4},{6,7},{7,6},{8,9},{9,8},{10,11... | collective-permute-start | bytes 811016 | tf_op jit(solution)/shard_map/ppermute | solution.py:426

commit v2 on v1

--- a/solution.py
+++ b/solution.py
@@ -166,9 +166,14 @@
         copy.start()
     which = lax.axis_index("ka")
     limits[...] = jnp.full(limits.shape, tolerance[which].astype(F32) / 8.0)
-    rows_out[...] = site_rows[...]
+    tile = chosen.shape[0]
+
+    def folded(position):
+        return jnp.where(position >= tile // 2, position - tile // 2, tile - 1 - position)
+
+    rows_out[...] = folded(site_rows[...])
     place = lax.broadcasted_iota(jnp.int32, chosen.shape, 0)
-    chosen[...] = jnp.where(place == site_cols[0], 1.0, 0.0).astype(BF16)
+    chosen[...] = jnp.where(place == folded(site_cols[0]), 1.0, 0.0).astype(BF16)
     for copy in copies:
         copy.wait()
 
@@ -186,6 +191,18 @@
     right = result[:, tile - HALO :]
     send_a[...] = jnp.where(even_col, right, left)
     send_b[...] = jnp.where(even_col, left, right)
+
+
+def fold_difference(x, axis):
+    half = x.shape[axis] // 2
+    sides = (lax.slice_in_dim(x, 0, half, axis=axis), lax.slice_in_dim(x, half, 2 * half, axis=axis))
+    out = []
+    for side, other in (sides, sides[::-1]):
+        first = lax.broadcasted_iota(jnp.int32, side.shape, axis) == 0
+        edge = lax.slice_in_dim(other, 0, 1, axis=axis)
+        inward = jnp.where(first, edge, pltpu.roll(side, 1, axis))
+        out.append(pltpu.roll(side, half - 1, axis) - inward)
+    return jnp.concatenate(out, axis=axis)
 
 
 def image_body(
@@ -224,8 +241,9 @@
     spec_re = quads[:BAND, :BAND] + quads[BAND:, BAND:]
     spec_im = quads[BAND:, :BAND] - quads[:BAND, BAND:]
     count = spec_own.shape[0]
-    sources = [(spec_own, k) for k in range(count)] + [(spec_other, k) for k in range(count)]
-    for number, (spec, k) in enumerate(sources):
+    image[...] = jnp.zeros(image.shape, F32)
+
+    def add_kernel(spec, k):
         kr = spec[k, 0]
         ki = spec[k, 1]
         product = jnp.concatenate(
@@ -256,17 +274,19 @@
         back_im = even_im - odd_re
         forth = forth_re * forth_re + forth_im * forth_im
         back = back_re * back_re + back_im * back_im
-        if number == 0:
-            image[:, :half] = forth
-            image[:, half:] = back
-        else:
-            image[:, :half] += forth
-            image[:, half:] += back
-    picture = sum(mm(unfold_rows[...], part) for part in reversed(terms(image[...])))
-    picture = sum(mm(part, unfold_cols[...]) for part in reversed(terms(picture)))
-    pack[:tile, :] = picture
-    grad_rows = (pltpu.roll(picture, tile - 1, 0) - pltpu.roll(picture, 1, 0)) * 0.5
-    grad_cols = (pltpu.roll(picture, tile - 1, 1) - pltpu.roll(picture, 1, 1)) * 0.5
+        image[:, :half] += forth
+        image[:, half:] += back
+
+    def add_kernels(step, carry):
+        for j in range(4):
+            add_kernel(spec_own, step * 4 + j)
+            add_kernel(spec_other, step * 4 + j)
+        return carry
+
+    lax.fori_loop(0, count // 4, add_kernels, 0)
+    picture = image[...]
+    grad_rows = fold_difference(picture, 0) * 0.5
+    grad_cols = fold_difference(picture, 1) * 0.5
     slope = jnp.sqrt(grad_rows * grad_rows + grad_cols * grad_cols)
     errors = terms((picture - LEVEL) / jnp.maximum(slope, SLOPE_FLOOR))
     sites = site_rows.shape[2]
@@ -288,6 +308,11 @@
             peak, shares = jnp.maximum(peak, size), shares + share
     lane = lax.broadcasted_iota(jnp.int32, stats.shape, 1)
     stats[...] = jnp.where(lane == 0, jnp.max(peak), jnp.sum(shares))
+
+    @pl.when(lax.axis_index("ka") == ITERS - 1)
+    def _():
+        plain = sum(mm(unfold_rows[...], part) for part in reversed(terms(image[...])))
+        pack[:tile, :] = sum(mm(part, unfold_cols[...]) for part in reversed(terms(plain)))
 
 
 def final_body(pack, other, stats, intensity, errors, peaks, shares, *, total):

time: 42.2 us -> 41.3 us (0.979)
  Pallas kernels: 17.5 us -> 16.5 us
    pallas_call x1, Pallas kernels: 9.35 us -> 8.39 us  [shards(): pl.pallas_call(image_body, out_shape=[shape(pack_rows, tile), shape(membe...]
where the time goes in v2:
time: 41.3 us; the launch traced here: 40.9 us
  Pallas kernels  16.5 us (40%)
  blocking collectives  10.4 us (25%)
  starting transfers between devices  8.24 us (20%)
  waiting for transfers between devices  4.44 us (11%)
  between operations  0.68 us (2%)
  local copies, waits for them, and re-layouts  0.66 us (2%)
    all_to_all x1, blocking collectives, shards(): merged = lax.all_to_all(stats, ('tx', 'ty', 'ka'), 0, 0, tiled=True)  10.4 us
    pallas_call x1, Pallas kernels, shards(): pl.pallas_call(image_body, out_shape=[shape(pack_rows, tile), shape(membe...  8.39 us
    ppermute x3, starting transfers between devices, neighbours(): got.append(lax.ppermute(sent, axis, pairs + [(b, a) for a, b in pairs]))  7.61 us
    ppermute x3, waiting for transfers between devices, neighbours(): got.append(lax.ppermute(sent, axis, pairs + [(b, a) for a, b in pairs]))  4.44 us
    pallas_call x1, Pallas kernels, shards(): pl.pallas_call(functools.partial(prepare_image_body, count=len(constants)...  2.28 us
    pallas_call x1, Pallas kernels, shards(): pl.pallas_call(strips_body, out_shape=[shape(tile, tile), shape(tile, til...  2.14 us
    pallas_call x1, Pallas kernels, shards(): pl.pallas_call(functools.partial(prepare_rows_body, count=len(fwd_rows)),...  1.89 us
    pallas_call x1, Pallas kernels, shards(): pl.pallas_call(rows_body, out_shape=[shape(half_rows, tile), shape(half_r...  1.08 us
  transfers between devices with their start and end apart: 5, of which 2 were waited for; matrix products, arithmetic and copies ran while one was open for 0% of the time, Pallas kernels for 8%

profile of v2, /device:TPU:0, one launch (start us, length us, event | category | flops | bytes accessed | tf_op | source)
XLA Modules:
  0.0 40.9 jit_solution(4451139292976220367)
XLA Ops:
  0.6 2.1 %strips.1 = (f32[256,256]{1,0:T(8,128)}, f32[256,256]{1,0:T(8,128)S(1)}, f32[128,256]{1,0:T(8,128)S(1)}, f32[128,256]{1,0:T(8,128)S(1)}) custom-call(f32[256,256]{1,0:T(8,128)} %mask.1, s32[1,1,512]{2,1,0:T(1,128)} %rows.2, s32[1,1,512]{2,1,0:T(1,128)} %cols.1, s32[1,1,512]{2,1,0:T(1,128)} %length.1, s32[1,1,512]{2,1,0:T(1,128)} %orient.1, ...), custom_call_target="tpu_custom_call" | custom-call | tf_op jit(solution)/shard_map/strips/pallas_call | solution.py:380
  2.8 0.0 copy-start
  2.8 0.7 %copy-done = f32[8]{0:T(128)S(1)} copy-done((f32[8]{0:T(128)S(1)}, f32[8]{0:T(128)}, u32[]{:S(2)}) %copy-start) | copy-done | bytes 56
  3.4 1.9 %prepare_rows.1 = (f32[8,2,128,128]{3,2,1,0:T(8,128)S(1)}, bf16[144,512]{1,0:T(8,128)(2,1)S(1)}, bf16[144,512]{1,0:T(8,128)(2,1)S(1)}, bf16[144,512]{1,0:T(8,128)(2,1)S(1)}) custom-call(f32[128,256]{1,0:T(8,128)S(1)} %get-tuple-element.37.anchor, f32[8]{0:T(128)S(1)} %copy-done, f32[8,2,128,128]{3,2,1,0:T(8,128)} %spectra.1, ...), custom_call_target="tpu_custom_call" | custom-call | tf_op jit(solution)/shard_map/prepare_rows/pallas_call | solution.py:389
  5.3 0.6 %collective-permute-start.3 = (f32[8,2,128,128]{3,2,1,0:T(8,128)S(1)}, f32[8,2,128,128]{3,2,1,0:T(8,128)S(1)}, u32[]{:S(2)}, u32[]{:S(2)}) collective-permute-start(f32[8,2,128,128]{3,2,1,0:T(8,128)S(1)} %get-tuple-element.44.spec_own), channel_id=1, source_target_pairs={{0,1},{1,0},{2,3},{3,2},{4,5},{5,4},{6,7},{7,6},{8,9},{9,8},{10,11... | collective-permute-start | bytes 3145736 | tf_op jit(solution)/shard_map/ppermute | solution.py:399
  5.9 0.7 %collective-permute-start.1 = (f32[128,256]{1,0:T(8,128)S(1)}, f32[128,256]{1,0:T(8,128)S(1)}, u32[]{:S(2)}, u32[]{:S(2)}) collective-permute-start(f32[128,256]{1,0:T(8,128)S(1)} %get-tuple-element.38), channel_id=1, source_target_pairs={{4,8},{8,4},{5,9},{9,5},{6,10},{10,6},{7,11},{11,7},{20,24},{24,20... | collective-permute-start | bytes 393224 | tf_op jit(solution)/shard_map/ppermute | solution.py:356
  6.5 5.5 %collective-permute-start = (f32[128,256]{1,0:T(8,128)S(1)}, f32[128,256]{1,0:T(8,128)S(1)}, u32[]{:S(2)}, u32[]{:S(2)}) collective-permute-start(f32[128,256]{1,0:T(8,128)S(1)} %get-tuple-element.37.anchor), channel_id=1, source_target_pairs={{0,4},{8,12},{4,0},{12,8},{1,5},{9,13},{5,1},{13,9},{2,6},{10,14},... | collective-permute-start | bytes 393224 | tf_op jit(solution)/shard_map/ppermute | solution.py:356
  12.0 0.0 collective-permute-done.1.got_b
  12.0 3.9 %collective-permute-done.got_a = f32[128,256]{1,0:T(8,128)S(1)} collective-permute-done((f32[128,256]{1,0:T(8,128)S(1)}, f32[128,256]{1,0:T(8,128)S(1)}, u32[]{:S(2)}, u32[]{:S(2)}) %collective-permute-start) | collective-permute-done | bytes 131104 | tf_op jit(solution)/shard_map/ppermute | solution.py:356
  15.9 1.1 %rows.3 = (f32[144,256]{1,0:T(8,128)S(1)}, f32[144,128]{1,0:T(8,128)S(1)}, f32[144,128]{1,0:T(8,128)}) custom-call(f32[256,256]{1,0:T(8,128)S(1)} %get-tuple-element.36.current, f32[128,256]{1,0:T(8,128)S(1)} %collective-permute-done.got_a, f32[128,256]{1,0:T(8,128)S(1)} %collective-permute-done.1.got_b, bf16[144,512]{1,0:T(8,128)(2,1)S(1)} %get-tuple-element.39.high, ...), custom_call_target="tpu_custom_call" | custom-call | tf_op jit(solution)/shard_map/rows/pallas_call | solution.py:400
  17.0 0.0 copy-start.1
  17.0 1.5 %collective-permute-start.2 = (f32[144,128]{1,0:T(8,128)S(1)}, f32[144,128]{1,0:T(8,128)S(1)}, u32[]{:S(2)}, u32[]{:S(2)}) collective-permute-start(f32[144,128]{1,0:T(8,128)S(1)} %get-tuple-element.43.refs_0_), channel_id=1, source_target_pairs={{0,2},{2,0},{1,3},{3,1},{4,6},{6,4},{5,7},{7,5},{8,10},{10,8},{9,1... | collective-permute-start | bytes 221192 | tf_op jit(solution)/shard_map/ppermute | solution.py:356
  18.4 0.0 copy-done.1
  18.5 2.3 %prepare_image.1 = (bf16[256,2048]{1,0:T(8,128)(2,1)S(1)}, s32[1,1,2048]{2,1,0:T(1,128)S(1)}, f32[8,128]{1,0:T(8,128)S(1)}, bf16[512,256]{1,0:T(8,128)(2,1)S(1)}...) custom-call(f32[144,128]{1,0:T(8,128)S(1)} %get-tuple-element.43.ref, ...), custom_call_target="tpu_custom_call" | custom-call | tf_op jit(solution)/shard_map/prepare_image/pallas_call | solution.py:410
  20.7 0.6 %collective-permute-done.2.got_a = f32[144,128]{1,0:T(8,128)S(1)} collective-permute-done((f32[144,128]{1,0:T(8,128)S(1)}, f32[144,128]{1,0:T(8,128)S(1)}, u32[]{:S(2)}, u32[]{:S(2)}) %collective-permute-start.2) | collective-permute-done | bytes 73760 | tf_op jit(solution)/shard_map/ppermute | solution.py:356
  21.3 0.0 collective-permute-done.3.spec_other
  21.3 8.4 %image.1 = (f32[264,256]{1,0:T(8,128)S(1)}, f32[16,128]{1,0:T(8,128)S(1)}) custom-call(f32[144,256]{1,0:T(8,128)S(1)} %get-tuple-element.42.mine, f32[144,128]{1,0:T(8,128)S(1)} %collective-permute-done.2.got_a, f32[144,128]{1,0:T(8,128)S(1)} %broadcast_in_dim.3.got_b, f32[8,2,128,128]{3,2,1,0:T(8,128)S(1)} %get-tuple-element.44.spec_own, ...), custom_call_target="tpu_custom_call" | custom-call | tf_op jit(solution)/shard_map/image/pallas_call | solution.py:432
  29.7 0.1 collective-permute-start.4
  29.8 10.4 %all_to_all.11 = f32[16,1,128]{2,1,0:T(1,128)S(1)} all-to-all(f32[16,1,128]{2,1,0:T(1,128)S(1)} %bitcast.5), channel_id=1, replica_groups=mesh['groups'=2,'tx'=4,'ty'=2,'ka'=2] {'tx','ty','ka'}, dimensions={0} | all-to-all | bytes 16384 | tf_op jit(solution)/shard_map/all_to_all | solution.py:452
  40.2 0.0 collective-permute-done.4.other
  40.2 0.8 %final.1 = (f32[256,256]{1,0:T(8,128)}, f32[1,1,2,2048]{3,2,1,0:T(2,128)}, f32[2]{0:T(128)}, f32[2]{0:T(128)}) custom-call(f32[264,256]{1,0:T(8,128)S(1)} %get-tuple-element.60.pack, f32[264,256]{1,0:T(8,128)S(1)} %collective-permute-done.4.other, f32[16,128]{1,0:T(8,128)S(1)} %bitcast.4), custom_call_target="tpu_custom_call" | custom-call | tf_op jit(solution)/shard_map/final/pallas_call | solution.py:454
  (1 shorter events, 0.0 us)
Async XLA Ops:
  2.8 0.7 %copy-start = (f32[8]{0:T(128)S(1)}, f32[8]{0:T(128)}, u32[]{:S(2)}) copy-start(f32[8]{0:T(128)} %weights.1) | copy-start | bytes 100
  5.3 16.0 %collective-permute-start.3 = (f32[8,2,128,128]{3,2,1,0:T(8,128)S(1)}, f32[8,2,128,128]{3,2,1,0:T(8,128)S(1)}, u32[]{:S(2)}, u32[]{:S(2)}) collective-permute-start(f32[8,2,128,128]{3,2,1,0:T(8,128)S(1)} %get-tuple-element.44.spec_own), channel_id=1, source_target_pairs={{0,1},{1,0},{2,3},{3,2},{4,5},{5,4},{6,7},{7,6},{8,9},{9,8},{10,11... | collective-permute-start | bytes 3145736 | tf_op jit(solution)/shard_map/ppermute | solution.py:399
  5.9 6.1 %collective-permute-start.1 = (f32[128,256]{1,0:T(8,128)S(1)}, f32[128,256]{1,0:T(8,128)S(1)}, u32[]{:S(2)}, u32[]{:S(2)}) collective-permute-start(f32[128,256]{1,0:T(8,128)S(1)} %get-tuple-element.38), channel_id=1, source_target_pairs={{4,8},{8,4},{5,9},{9,5},{6,10},{10,6},{7,11},{11,7},{20,24},{24,20... | collective-permute-start | bytes 393224 | tf_op jit(solution)/shard_map/ppermute | solution.py:356
  6.5 9.3 %collective-permute-start = (f32[128,256]{1,0:T(8,128)S(1)}, f32[128,256]{1,0:T(8,128)S(1)}, u32[]{:S(2)}, u32[]{:S(2)}) collective-permute-start(f32[128,256]{1,0:T(8,128)S(1)} %get-tuple-element.37.anchor), channel_id=1, source_target_pairs={{0,4},{8,12},{4,0},{12,8},{1,5},{9,13},{5,1},{13,9},{2,6},{10,14},... | collective-permute-start | bytes 393224 | tf_op jit(solution)/shard_map/ppermute | solution.py:356
  17.0 1.5 %copy-start.1 = (s32[2]{0:T(128)S(1)}, s32[2]{0:T(128)}, u32[]{:S(2)}) copy-start(s32[2]{0:T(128)} %refs_1_.2) | copy-start | bytes 28
  17.0 4.4 %collective-permute-start.2 = (f32[144,128]{1,0:T(8,128)S(1)}, f32[144,128]{1,0:T(8,128)S(1)}, u32[]{:S(2)}, u32[]{:S(2)}) collective-permute-start(f32[144,128]{1,0:T(8,128)S(1)} %get-tuple-element.43.refs_0_), channel_id=1, source_target_pairs={{0,2},{2,0},{1,3},{3,1},{4,6},{6,4},{5,7},{7,5},{8,10},{10,8},{9,1... | collective-permute-start | bytes 221192 | tf_op jit(solution)/shard_map/ppermute | solution.py:356
  29.7 10.5 %collective-permute-start.4 = (f32[264,256]{1,0:T(8,128)S(1)}, f32[264,256]{1,0:T(8,128)S(1)}, u32[]{:S(2)}, u32[]{:S(2)}) collective-permute-start(f32[264,256]{1,0:T(8,128)S(1)} %get-tuple-element.60.pack), channel_id=1, source_target_pairs={{0,1},{1,0},{2,3},{3,2},{4,5},{5,4},{6,7},{7,6},{8,9},{9,8},{10,11... | collective-permute-start | bytes 811016 | tf_op jit(solution)/shard_map/ppermute | solution.py:451

commit v3 on v2

--- a/solution.py
+++ b/solution.py
@@ -92,44 +92,54 @@
     return small + mm(a[1], b[0]) + mm(a[0], b[1]) + mm(a[0], b[0])
 
 
-def strips_body(mask, rows, cols, length, orient, moves, corrected, current, send_a, send_b):
-    tile = mask.shape[0]
-    frags = rows.shape[2]
-    first = lax.axis_index("ka") == 0
-    even = lax.axis_index("tx") % 2 == 0
-    place = lax.broadcasted_iota(jnp.int32, (tile, frags), 0)
+def strip_sum(rows, cols, length, orient, moves, iteration, tile):
+    place = lax.broadcasted_iota(jnp.int32, (tile, rows.shape[2]), 0)
     row_start = rows[0]
     col_start = cols[0]
     size = length[0]
     along_rows = orient[0] == 0
-    state = mask[...]
-    states = []
-    for iteration in range(ITERS):
-        shift = moves[0, 0, iteration : iteration + 1, :]
-        lower = jnp.minimum(shift, 0)
-        upper = jnp.maximum(shift, 0)
-        row_low = jnp.where(along_rows, row_start, row_start + lower)
-        row_high = jnp.where(along_rows, row_start + size, row_start + upper)
-        col_low = jnp.where(along_rows, col_start + lower, col_start)
-        col_high = jnp.where(along_rows, col_start + upper, col_start + size)
-        sign = jnp.where(shift > 0, 1.0, jnp.where(shift < 0, -1.0, 0.0))
-        in_rows = jnp.where((place >= row_low) & (place < row_high), sign, 0.0)
-        in_cols = jnp.where((place >= col_low) & (place < col_high), 1.0, 0.0)
-        strips = lax.dot_general(
-            in_rows.astype(BF16),
-            in_cols.astype(BF16),
-            (((1,), (1,)), ((), ())),
-            preferred_element_type=F32,
-        )
-        state = jnp.clip(state + strips, 0.0, 1.0)
-        states.append(state)
-    corrected[...] = states[1]
-    mine = jnp.where(first, states[0], states[1])
-    current[...] = mine
-    top = mine[:HALO]
-    bottom = mine[tile - HALO :]
+    shift = moves[0, 0, iteration : iteration + 1, :]
+    lower = jnp.minimum(shift, 0)
+    upper = jnp.maximum(shift, 0)
+    row_low = jnp.where(along_rows, row_start, row_start + lower)
+    row_high = jnp.where(along_rows, row_start + size, row_start + upper)
+    col_low = jnp.where(along_rows, col_start + lower, col_start)
+    col_high = jnp.where(along_rows, col_start + upper, col_start + size)
+    sign = jnp.where(shift > 0, 1.0, jnp.where(shift < 0, -1.0, 0.0))
+    in_rows = jnp.where((place >= row_low) & (place < row_high), sign, 0.0)
+    in_cols = jnp.where((place >= col_low) & (place < col_high), 1.0, 0.0)
+    return lax.dot_general(
+        in_rows.astype(BF16),
+        in_cols.astype(BF16),
+        (((1,), (1,)), ((), ())),
+        preferred_element_type=F32,
+    )
+
+
+def strips_body(mask, rows, cols, length, orient, moves, current, send_a, send_b):
+    tile = mask.shape[0]
+    even = lax.axis_index("tx") % 2 == 0
+    frags = (rows, cols, length, orient, moves)
+    current[...] = jnp.clip(mask[...] + strip_sum(*frags, 0, tile), 0.0, 1.0)
+
+    @pl.when(lax.axis_index("ka") == ITERS - 1)
+    def _():
+        current[...] = jnp.clip(current[...] + strip_sum(*frags, 1, tile), 0.0, 1.0)
+
+    top = current[:HALO]
+    bottom = current[tile - HALO :]
     send_a[...] = jnp.where(even, bottom, top)
     send_b[...] = jnp.where(even, top, bottom)
+
+
+def corrected_body(current, anchor, rows, cols, length, orient, moves, corrected):
+    tile = current.shape[0]
+    corrected[...] = current[...]
+
+    @pl.when(lax.axis_index("ka") == 0)
+    def _():
+        frags = (rows, cols, length, orient, moves)
+        corrected[...] = jnp.clip(current[...] + strip_sum(*frags, 1, tile), 0.0, 1.0)
 
 
 def prepare_rows_body(anchor, weights, spectra, *refs, count):
@@ -377,14 +387,23 @@
     fwd_rows, fwd_cols, expand, inv_rows, inv_cols, unfold = tables(tile)
     half_rows = fwd_rows[0].shape[0]
     swap = [(0, 1), (1, 0)]
-    corrected, current, send_a, send_b = pl.pallas_call(
+    frags = [in_hbm(x) for x in (frag_rows, frag_cols, frag_length, frag_orient, frag_moves)]
+    current, send_a, send_b = pl.pallas_call(
         strips_body,
-        out_shape=[shape(tile, tile), shape(tile, tile), shape(HALO, tile), shape(HALO, tile)],
+        out_shape=[shape(tile, tile), shape(HALO, tile), shape(HALO, tile)],
         in_specs=spec(6),
-        out_specs=spec(4),
+        out_specs=spec(3),
         compiler_params=LIMIT,
         name="strips",
-    )(*map(in_hbm, (mask_raster, frag_rows, frag_cols, frag_length, frag_orient, frag_moves)))
+    )(in_hbm(mask_raster), *frags)
+    corrected = pl.pallas_call(
+        corrected_body,
+        out_shape=shape(tile, tile),
+        in_specs=spec(1) + spec(1, pl.ANY) + spec(5),
+        out_specs=spec(1)[0],
+        compiler_params=LIMIT,
+        name="corrected",
+    )(current, send_a, *frags)
     got_a, got_b = neighbours("tx", send_a, send_b)
     scaled, *row_tables = pl.pallas_call(
         functools.partial(prepare_rows_body, count=len(fwd_rows)),

time: 41.3 us -> 41.1 us (level)
  blocking collectives: 10.4 us -> 0 us
  waiting for transfers between devices: 4.44 us -> 8.95 us
  starting transfers between devices: 8.24 us -> 12.4 us
  Pallas kernels: 16.5 us -> 18 us
    all_to_all x1 -> x0, blocking collectives: 10.4 us -> none  [shards(): merged = lax.all_to_all(stats, ('tx', 'ty', 'ka'), 0, 0, tiled=True)]
    all_to_all x0 -> x1, waiting for transfers between devices: none -> 4.6 us  [shards(): merged = lax.all_to_all(stats, ('tx', 'ty', 'ka'), 0, 0, tiled=True)]
    all_to_all x0 -> x1, starting transfers between devices: none -> 4.16 us  [shards(): merged = lax.all_to_all(stats, ('tx', 'ty', 'ka'), 0, 0, tiled=True)]
    pallas_call x1 -> x2, Pallas kernels: 2.14 us -> 3.06 us  [the longest x1 1.75 us: shards(): pl.pallas_call(corrected_body, out_shape=shape(tile, tile), in_specs=spec...]
    pallas_call x1, Pallas kernels: 8.39 us -> 8.96 us  [shards(): pl.pallas_call(image_body, out_shape=[shape(pack_rows, tile), shape(membe...]
  transfers between devices with their start and end apart: 5 -> 6, of which waited for: 2 -> 3; matrix products, arithmetic and copies ran while one was open for 0% -> 0% of each run, Pallas kernels for 8% -> 13%
where the time goes in v3:
time: 41.1 us; the launch traced here: 40.8 us
  Pallas kernels  18 us (44%)
  starting transfers between devices  12.4 us (30%)
  waiting for transfers between devices  8.95 us (22%)
  between operations  0.69 us (2%)
  local copies, waits for them, and re-layouts  0.66 us (2%)
    pallas_call x1, Pallas kernels, shards(): pl.pallas_call(image_body, out_shape=[shape(pack_rows, tile), shape(membe...  8.96 us
    ppermute x3, starting transfers between devices, neighbours(): got.append(lax.ppermute(sent, axis, pairs + [(b, a) for a, b in pairs]))  7.42 us
    all_to_all x1, waiting for transfers between devices, shards(): merged = lax.all_to_all(stats, ('tx', 'ty', 'ka'), 0, 0, tiled=True)  4.6 us
    ppermute x3, waiting for transfers between devices, neighbours(): got.append(lax.ppermute(sent, axis, pairs + [(b, a) for a, b in pairs]))  4.34 us
    all_to_all x1, starting transfers between devices, shards(): merged = lax.all_to_all(stats, ('tx', 'ty', 'ka'), 0, 0, tiled=True)  4.16 us
    pallas_call x1, Pallas kernels, shards(): pl.pallas_call(functools.partial(prepare_image_body, count=len(constants)...  2.28 us
    pallas_call x1, Pallas kernels, shards(): pl.pallas_call(functools.partial(prepare_rows_body, count=len(fwd_rows)),...  1.89 us
    pallas_call x1, Pallas kernels, shards(): pl.pallas_call(corrected_body, out_shape=shape(tile, tile), in_specs=spec...  1.75 us
  transfers between devices with their start and end apart: 6, of which 3 were waited for; matrix products, arithmetic and copies ran while one was open for 0% of the time, Pallas kernels for 13%

profile of v3, /device:TPU:0, one launch (start us, length us, event | category | flops | bytes accessed | tf_op | source)
XLA Modules:
  0.0 40.8 jit_solution(3959277825964068287)
XLA Ops:
  0.6 1.3 %strips.1 = (f32[256,256]{1,0:T(8,128)S(1)}, f32[128,256]{1,0:T(8,128)S(1)}, f32[128,256]{1,0:T(8,128)S(1)}) custom-call(f32[256,256]{1,0:T(8,128)} %mask.1, s32[1,1,512]{2,1,0:T(1,128)} %rows.5, s32[1,1,512]{2,1,0:T(1,128)} %cols.3, s32[1,1,512]{2,1,0:T(1,128)} %length.3, s32[1,1,512]{2,1,0:T(1,128)} %orient.3, s32[1,1,2,512]{3,2,1,0:T(2,128)} %moves.3), custom_call_target="tpu_custom_call" | custom-call | tf_op jit(solution)/shard_map/strips/pallas_call | solution.py:391
  1.9 0.0 copy-start
  2.0 0.6 %copy-done = f32[8]{0:T(128)S(1)} copy-done((f32[8]{0:T(128)S(1)}, f32[8]{0:T(128)}, u32[]{:S(2)}) %copy-start) | copy-done | bytes 56
  2.6 1.9 %prepare_rows.1 = (f32[8,2,128,128]{3,2,1,0:T(8,128)S(1)}, bf16[144,512]{1,0:T(8,128)(2,1)S(1)}, bf16[144,512]{1,0:T(8,128)(2,1)S(1)}, bf16[144,512]{1,0:T(8,128)(2,1)S(1)}) custom-call(f32[128,256]{1,0:T(8,128)S(1)} %get-tuple-element.36.anchor, f32[8]{0:T(128)S(1)} %copy-done, f32[8,2,128,128]{3,2,1,0:T(8,128)} %spectra.1, ...), custom_call_target="tpu_custom_call" | custom-call | tf_op jit(solution)/shard_map/prepare_rows/pallas_call | solution.py:408
  4.5 0.8 %collective-permute-start.3 = (f32[8,2,128,128]{3,2,1,0:T(8,128)S(1)}, f32[8,2,128,128]{3,2,1,0:T(8,128)S(1)}, u32[]{:S(2)}, u32[]{:S(2)}) collective-permute-start(f32[8,2,128,128]{3,2,1,0:T(8,128)S(1)} %get-tuple-element.43.spec_own), channel_id=1, source_target_pairs={{0,1},{1,0},{2,3},{3,2},{4,5},{5,4},{6,7},{7,6},{8,9},{9,8},{10,11... | collective-permute-start | bytes 3145736 | tf_op jit(solution)/shard_map/ppermute | solution.py:418
  5.3 0.7 %collective-permute-start.1 = (f32[128,256]{1,0:T(8,128)S(1)}, f32[128,256]{1,0:T(8,128)S(1)}, u32[]{:S(2)}, u32[]{:S(2)}) collective-permute-start(f32[128,256]{1,0:T(8,128)S(1)} %get-tuple-element.37), channel_id=1, source_target_pairs={{4,8},{8,4},{5,9},{9,5},{6,10},{10,6},{7,11},{11,7},{20,24},{24,20... | collective-permute-start | bytes 393224 | tf_op jit(solution)/shard_map/ppermute | solution.py:366
  6.0 5.3 %collective-permute-start = (f32[128,256]{1,0:T(8,128)S(1)}, f32[128,256]{1,0:T(8,128)S(1)}, u32[]{:S(2)}, u32[]{:S(2)}) collective-permute-start(f32[128,256]{1,0:T(8,128)S(1)} %get-tuple-element.36.anchor), channel_id=1, source_target_pairs={{0,4},{8,12},{4,0},{12,8},{1,5},{9,13},{5,1},{13,9},{2,6},{10,14},... | collective-permute-start | bytes 393224 | tf_op jit(solution)/shard_map/ppermute | solution.py:366
  11.3 0.0 collective-permute-done.1.got_b
  11.3 3.8 %collective-permute-done.got_a = f32[128,256]{1,0:T(8,128)S(1)} collective-permute-done((f32[128,256]{1,0:T(8,128)S(1)}, f32[128,256]{1,0:T(8,128)S(1)}, u32[]{:S(2)}, u32[]{:S(2)}) %collective-permute-start) | collective-permute-done | bytes 131104 | tf_op jit(solution)/shard_map/ppermute | solution.py:366
  15.1 1.1 %rows.4 = (f32[144,256]{1,0:T(8,128)S(1)}, f32[144,128]{1,0:T(8,128)S(1)}, f32[144,128]{1,0:T(8,128)}) custom-call(f32[256,256]{1,0:T(8,128)S(1)} %get-tuple-element.35.current, f32[128,256]{1,0:T(8,128)S(1)} %collective-permute-done.got_a, f32[128,256]{1,0:T(8,128)S(1)} %collective-permute-done.1.got_b, bf16[144,512]{1,0:T(8,128)(2,1)S(1)} %get-tuple-element.38.high, ...), custom_call_target="tpu_custom_call" | custom-call | tf_op jit(solution)/shard_map/rows/pallas_call | solution.py:419
  16.1 0.0 copy-start.1
  16.1 1.5 %collective-permute-start.2 = (f32[144,128]{1,0:T(8,128)S(1)}, f32[144,128]{1,0:T(8,128)S(1)}, u32[]{:S(2)}, u32[]{:S(2)}) collective-permute-start(f32[144,128]{1,0:T(8,128)S(1)} %get-tuple-element.42.refs_0_), channel_id=1, source_target_pairs={{0,2},{2,0},{1,3},{3,1},{4,6},{6,4},{5,7},{7,5},{8,10},{10,8},{9,1... | collective-permute-start | bytes 221192 | tf_op jit(solution)/shard_map/ppermute | solution.py:366
  17.6 0.0 copy-done.1
  17.6 2.3 %prepare_image.1 = (bf16[256,2048]{1,0:T(8,128)(2,1)S(1)}, s32[1,1,2048]{2,1,0:T(1,128)S(1)}, f32[8,128]{1,0:T(8,128)S(1)}, bf16[512,256]{1,0:T(8,128)(2,1)S(1)}...) custom-call(f32[144,128]{1,0:T(8,128)S(1)} %get-tuple-element.42.ref, ...), custom_call_target="tpu_custom_call" | custom-call | tf_op jit(solution)/shard_map/prepare_image/pallas_call | solution.py:429
  19.9 0.6 %collective-permute-done.2.got_a = f32[144,128]{1,0:T(8,128)S(1)} collective-permute-done((f32[144,128]{1,0:T(8,128)S(1)}, f32[144,128]{1,0:T(8,128)S(1)}, u32[]{:S(2)}, u32[]{:S(2)}) %collective-permute-start.2) | collective-permute-done | bytes 73760 | tf_op jit(solution)/shard_map/ppermute | solution.py:366
  20.5 0.0 collective-permute-done.3.spec_other
  20.5 9.0 %image.1 = (f32[264,256]{1,0:T(8,128)S(1)}, f32[16,128]{1,0:T(8,128)}) custom-call(f32[144,256]{1,0:T(8,128)S(1)} %get-tuple-element.41.mine, f32[144,128]{1,0:T(8,128)S(1)} %collective-permute-done.2.got_a, f32[144,128]{1,0:T(8,128)S(1)} %broadcast_in_dim.3.got_b, f32[8,2,128,128]{3,2,1,0:T(8,128)S(1)} %get-tuple-element.43.spec_own, ...), custom_call_target="tpu_custom_call" | custom-call | tf_op jit(solution)/shard_map/image/pallas_call | solution.py:451
  29.5 0.0 collective-permute-start.4
  29.5 4.2 %all-to-all-start = ((f32[16,1,128]{2,1,0:T(1,128)}), f32[16,1,128]{2,1,0:T(1,128)S(1)}, u32[]{:S(2)}, u32[]{:S(2)}) async-start(f32[16,1,128]{2,1,0:T(1,128)} %bitcast.1), calls=%async_computation | async-start | bytes 16384 | tf_op jit(solution)/shard_map/all_to_all | solution.py:471
  33.6 1.8 %corrected.1 = f32[256,256]{1,0:T(8,128)} custom-call(f32[256,256]{1,0:T(8,128)S(1)} %get-tuple-element.35.current, f32[128,256]{1,0:T(8,128)S(1)} %get-tuple-element.36.anchor, s32[1,1,512]{2,1,0:T(1,128)} %rows.5, s32[1,1,512]{2,1,0:T(1,128)} %cols.3, s32[1,1,512]{2,1,0:T(1,128)} %length.3, s32[1,1,512]{2,1,0:T(1,128)} %orient.3, s32[1,1,2,512]{3,2,1,0:T(2,128)} %moves.3), custom_call_target="tpu_custom_call" | custom-call | tf_op jit(solution)/shard_map/corrected/pallas_call | solution.py:399
  35.4 4.6 %all-to-all-done = f32[16,1,128]{2,1,0:T(1,128)S(1)} async-done(((f32[16,1,128]{2,1,0:T(1,128)}), f32[16,1,128]{2,1,0:T(1,128)S(1)}, u32[]{:S(2)}, u32[]{:S(2)}) %all-to-all-start) | async-done | bytes 8224 | tf_op jit(solution)/shard_map/all_to_all | solution.py:471
  40.0 0.0 collective-permute-done.4.other
  40.0 0.8 %final.1 = (f32[256,256]{1,0:T(8,128)}, f32[1,1,2,2048]{3,2,1,0:T(2,128)}, f32[2]{0:T(128)}, f32[2]{0:T(128)}) custom-call(f32[264,256]{1,0:T(8,128)S(1)} %get-tuple-element.59.pack, f32[264,256]{1,0:T(8,128)S(1)} %collective-permute-done.4.other, f32[16,128]{1,0:T(8,128)S(1)} %bitcast.4), custom_call_target="tpu_custom_call" | custom-call | tf_op jit(solution)/shard_map/final/pallas_call | solution.py:473
  (1 shorter events, 0.0 us)
Async XLA Ops:
  1.9 0.7 %copy-start = (f32[8]{0:T(128)S(1)}, f32[8]{0:T(128)}, u32[]{:S(2)}) copy-start(f32[8]{0:T(128)} %weights.1) | copy-start | bytes 100
  4.5 16.0 %collective-permute-start.3 = (f32[8,2,128,128]{3,2,1,0:T(8,128)S(1)}, f32[8,2,128,128]{3,2,1,0:T(8,128)S(1)}, u32[]{:S(2)}, u32[]{:S(2)}) collective-permute-start(f32[8,2,128,128]{3,2,1,0:T(8,128)S(1)} %get-tuple-element.43.spec_own), channel_id=1, source_target_pairs={{0,1},{1,0},{2,3},{3,2},{4,5},{5,4},{6,7},{7,6},{8,9},{9,8},{10,11... | collective-permute-start | bytes 3145736 | tf_op jit(solution)/shard_map/ppermute | solution.py:418
  5.3 5.9 %collective-permute-start.1 = (f32[128,256]{1,0:T(8,128)S(1)}, f32[128,256]{1,0:T(8,128)S(1)}, u32[]{:S(2)}, u32[]{:S(2)}) collective-permute-start(f32[128,256]{1,0:T(8,128)S(1)} %get-tuple-element.37), channel_id=1, source_target_pairs={{4,8},{8,4},{5,9},{9,5},{6,10},{10,6},{7,11},{11,7},{20,24},{24,20... | collective-permute-start | bytes 393224 | tf_op jit(solution)/shard_map/ppermute | solution.py:366
  6.0 9.0 %collective-permute-start = (f32[128,256]{1,0:T(8,128)S(1)}, f32[128,256]{1,0:T(8,128)S(1)}, u32[]{:S(2)}, u32[]{:S(2)}) collective-permute-start(f32[128,256]{1,0:T(8,128)S(1)} %get-tuple-element.36.anchor), channel_id=1, source_target_pairs={{0,4},{8,12},{4,0},{12,8},{1,5},{9,13},{5,1},{13,9},{2,6},{10,14},... | collective-permute-start | bytes 393224 | tf_op jit(solution)/shard_map/ppermute | solution.py:366
  16.1 1.5 %copy-start.1 = (s32[2]{0:T(128)S(1)}, s32[2]{0:T(128)}, u32[]{:S(2)}) copy-start(s32[2]{0:T(128)} %refs_1_.2) | copy-start | bytes 28
  16.1 4.4 %collective-permute-start.2 = (f32[144,128]{1,0:T(8,128)S(1)}, f32[144,128]{1,0:T(8,128)S(1)}, u32[]{:S(2)}, u32[]{:S(2)}) collective-permute-start(f32[144,128]{1,0:T(8,128)S(1)} %get-tuple-element.42.refs_0_), channel_id=1, source_target_pairs={{0,2},{2,0},{1,3},{3,1},{4,6},{6,4},{5,7},{7,5},{8,10},{10,8},{9,1... | collective-permute-start | bytes 221192 | tf_op jit(solution)/shard_map/ppermute | solution.py:366
  29.5 10.5 %collective-permute-start.4 = (f32[264,256]{1,0:T(8,128)S(1)}, f32[264,256]{1,0:T(8,128)S(1)}, u32[]{:S(2)}, u32[]{:S(2)}) collective-permute-start(f32[264,256]{1,0:T(8,128)S(1)} %get-tuple-element.59.pack), channel_id=1, source_target_pairs={{0,1},{1,0},{2,3},{3,2},{4,5},{5,4},{6,7},{7,6},{8,9},{9,8},{10,11... | collective-permute-start | bytes 811016 | tf_op jit(solution)/shard_map/ppermute | solution.py:470
  29.5 10.5 %all-to-all-start = ((f32[16,1,128]{2,1,0:T(1,128)}), f32[16,1,128]{2,1,0:T(1,128)S(1)}, u32[]{:S(2)}, u32[]{:S(2)}) async-start(f32[16,1,128]{2,1,0:T(1,128)} %bitcast.1), calls=%async_computation | async-start | bytes 16384 | tf_op jit(solution)/shard_map/all_to_all | solution.py:471
